TPU v7x, 128 devices: a whole 4x4x4 slice. The times are simulated.
128 devices in a mesh: dp: 8 (over x, core), tensor: 16 (over z, y).
Axes of the slice: x: 4, y: 4, z: 4, core: 2. Of those that a mesh axis runs over, the one named last changes fastest.
Arguments:
- head_outputs: bfloat16 [16384, 4096], P('dp', 'tensor'), may hold values from -6 to 6
- out_weight: bfloat16 [4096, 4096], P('tensor'), may hold values from -0.09375 to 0.09375
- residual: bfloat16 [16384, 4096], P(('dp', 'tensor')), may hold values from -6 to 6
- norm_gain: float32 [4096], replicated, may hold values from 0.25 to 1.75
- chosen: int32 [64, 256], replicated, may hold values from 0 to 16383, as said below
- gates: float32 [64, 256], replicated, may hold values from 0.25 to 1
- place: int32 [64], replicated, may hold values from 0 to 63, each once
- w_gate: bfloat16 [128, 704, 4096], P(('dp', 'tensor')), may hold values from -0.09375 to 0.09375
- w_up: bfloat16 [128, 704, 4096], P(('dp', 'tensor')), may hold values from -0.09375 to 0.09375
- w_down: bfloat16 [128, 704, 4096], P(('dp', 'tensor')), may hold values from -0.15625 to 0.15625
Outputs:
- mixed: bfloat16 [16384, 4096], P(('dp', 'tensor'))
Inputs may be any that keep to these rules, and one draw needn't show every extreme that they name: `chosen`: row e lists 256 different tokens; at most 4 of them lie in one aligned block of 128 rows (the rows of one device), and in every row some block holds exactly 4.
All inputs are finite; a program needn't handle non-finite values.
Results may differ from a plain program's by a relative error of at most 0.012.
Values may be sent and summed in bfloat16 or wider, within the bound.
No kernel may reach another device: no remote copies, remote signals or barrier semaphores. Data moves between devices by JAX's collectives and lax.ppermute only.
A program may use at most 128 MiB of HBM per device.

v0:
```python
import jax
import jax.numpy as jnp
from jax import lax
from jax.sharding import PartitionSpec as P


def items_in_groups(x, axis, split_dim, concat_dim, work, item_dim, out_dim):

    def moved(group):
        return lax.all_to_all(group, axis, split_axis=split_dim, concat_axis=concat_dim, tiled=True)

    items = jax.tree.leaves(x)[0].shape[item_dim]
    ends = [items * k // 2 for k in range(2 + 1)] if items % 2 == 0 else [0, items]
    groups = [
        jax.tree.map(lambda a: lax.slice_in_dim(a, low, high, axis=item_dim), x)
        for low, high in zip(ends, ends[1:])
    ]
    arrived = [moved(group) for group in groups]
    made = [work(group) for group in arrived]
    return jax.tree.map(lambda *parts: jnp.concatenate(parts, axis=out_dim), *made)


def on_device(
    head_outputs, out_weight, residual, norm_gain, chosen, gates, place, w_gate, w_up, w_down
):
    tensor_count = lax.axis_size("tensor")
    replica_count = lax.axis_size("dp")
    owners = replica_count * tensor_count
    my_index = lax.axis_index("dp") * tensor_count + lax.axis_index("tensor")
    row_count = residual.shape[0]
    model_width = residual.shape[1]
    projected = lax.psum_scatter(
        jnp.dot(head_outputs, out_weight, preferred_element_type=jnp.float32).astype(jnp.bfloat16),
        "tensor",
        scatter_dimension=0,
        tiled=True,
    ).astype(jnp.float32)
    layer_state = residual.astype(jnp.float32) + projected
    scale = lax.rsqrt(jnp.mean(layer_state * layer_state, axis=1, keepdims=True) + 1.0)
    normed = (layer_state * scale * norm_gain[None, :]).astype(jnp.bfloat16)
    experts = place.shape[0]
    capacity = chosen.shape[1]
    most = 2 * capacity // owners
    pair_map = (place[None, :] == jnp.arange(experts, dtype=jnp.int32)[:, None]).astype(jnp.float32)
    chosen_pair = jnp.dot(
        pair_map, chosen.astype(jnp.float32), precision=lax.Precision.HIGHEST
    ).astype(jnp.int32)
    gates_pair = jnp.dot(pair_map, gates, precision=lax.Precision.HIGHEST)
    local_row = chosen_pair - my_index * row_count
    is_mine = (local_row >= 0) & (local_row < row_count)
    mine_float = is_mine.astype(jnp.float32)
    capacity_ids = jnp.arange(capacity, dtype=jnp.int32)
    earlier = (capacity_ids[:, None] < capacity_ids[None, :]).astype(jnp.float32)
    slot_rank = jnp.dot(mine_float, earlier, precision=lax.Precision.HIGHEST).astype(jnp.int32)
    matches = is_mine[:, :, None] & (
        slot_rank[:, :, None] == jnp.arange(most, dtype=jnp.int32)[None, None, :]
    )
    match_count = matches.astype(jnp.int32)
    send_row = jnp.sum(match_count * local_row[:, :, None], axis=1)
    send_valid = jnp.sum(match_count, axis=1) > 0
    send_gate = jnp.sum(jnp.where(matches, gates_pair[:, :, None], 0.0), axis=1)
    targets = send_row.reshape(-1)
    valid_flat = send_valid.reshape(-1)
    row_ids = jnp.arange(row_count, dtype=jnp.int32)
    selector = ((targets[:, None] == row_ids[None, :]) & valid_flat[:, None]).astype(jnp.bfloat16)
    picked = jnp.dot(selector, normed, preferred_element_type=jnp.float32).astype(jnp.bfloat16)
    picked = picked.reshape(experts, most, model_width)
    outgoing = jnp.broadcast_to(picked[:, None], (experts, 2, most, model_width)).reshape(
        owners, most, model_width
    )

    def run_expert(received):
        layout = received.shape
        flat = received.reshape(-1, layout[-1])
        contract = (((1,), (1,)), ((), ()))
        gate_part = lax.dot_general(flat, w_gate[0], contract, preferred_element_type=jnp.float32)
        up_part = lax.dot_general(flat, w_up[0], contract, preferred_element_type=jnp.float32)
        hidden = (jax.nn.silu(gate_part) * up_part).astype(jnp.bfloat16)
        result = jnp.dot(hidden, w_down[0], preferred_element_type=jnp.float32).astype(jnp.bfloat16)
        return result.reshape(layout)

    def serve(received):
        return lax.all_to_all(
            run_expert(received), ("dp", "tensor"), split_axis=0, concat_axis=0, tiled=True
        )

    returned = items_in_groups(outgoing, ("dp", "tensor"), 0, 0, serve, 1, 1)
    halves = returned.reshape(experts, 2, most, model_width).astype(jnp.float32)
    summed = (halves[:, 0] + halves[:, 1]).reshape(experts * most, model_width)
    combine = jnp.where(
        (targets[None, :] == row_ids[:, None]) & valid_flat[None, :],
        send_gate.reshape(-1)[None, :],
        0.0,
    )
    moe = jnp.dot(combine, summed, precision=lax.Precision.HIGHEST)
    return (layer_state + moe).astype(jnp.bfloat16)


def solution(mesh):
    return jax.shard_map(
        on_device,
        mesh=mesh,
        in_specs=(
            P("dp", "tensor"),
            P("tensor", None),
            P(("dp", "tensor"), None),
            P(),
            P(),
            P(),
            P(),
            P(("dp", "tensor"), None, None),
            P(("dp", "tensor"), None, None),
            P(("dp", "tensor"), None, None),
        ),
        out_specs=P(("dp", "tensor"), None),
        check_vma=False,
    )
```

profile of v0, /device:TPU:103, one launch (start us, length us, event | category | flops | bytes accessed | tf_op | source)
XLA Modules:
  0.0 311.3 jit_solution(8795632467001905463)
XLA Ops:
  6.5 1.6 copy-done
  8.1 9.4 %convolution_convert_fusion = bf16[2048,4096]{1,0:T(8,128)(2,1)} fusion(bf16[2048,256]{1,0:T(8,128)(2,1)} %param.10, bf16[256,4096]{1,0:T(8,128)(2,1)S(1)} %copy-done), kind=kOutput, calls=%fused_computation | convolution fusion | flops 4303355904 | bytes 19922944 | tf_op jit(solution)/shard_map/dot_general | solution.py:33
  17.5 0.6 copy-done.7
  18.2 0.2 copy-done.8
  18.4 0.2 compare_and_fusion
  18.7 0.2 convert_reduce_fusion
  19.4 109.8 %reduce-scatter.2.cloned.1.call-done = bf16[128,4096]{1,0:T(8,128)(2,1)} async-done(((bf16[2048,4096]{1,0:T(8,128)(2,1)}), bf16[128,4096]{1,0:T(8,128)(2,1)}) %reduce-scatter.2.cloned.1.call-update) | async-done | bytes 1048592 | tf_op jit(solution)/shard_map/reduce_scatter | solution.py:32
  129.2 1.7 multiply_reduce_fusion
  131.0 2.2 convolution_convert_fusion.1
  133.1 2.7 broadcast_in_dim.51
  135.9 2.1 broadcast_in_dim.52
  138.0 3.8 %fusion.59 = (bf16[128,2,4096]{2,1,0:T(2,128)(2,1)}, bf16[128,2,4096]{2,1,0:T(2,128)(2,1)S(1)}) fusion(bf16[128,4,4096]{2,1,0:T(4,128)(2,1)S(1)} %bitcast.44), kind=kLoop, calls=%fused_computation.62 | loop fusion | bytes 8388608 | tf_op jit(solution)/shard_map/slice | solution.py:15
  141.8 34.2 %all_to_all.20 = bf16[128,2,4096]{2,1,0:T(2,128)(2,1)} all-to-all(bf16[128,2,4096]{2,1,0:T(2,128)(2,1)S(1)} %get-tuple-element.8), channel_id=1, replica_groups=mesh['dp'=8,'tensor'=16] {'dp','tensor'}, dimensions={0} | all-to-all | bytes 4194304 | tf_op jit(solution)/shard_map/all_to_all | solution.py:10
  176.0 8.9 %all-to-all-start = ((bf16[128,2,4096]{2,1,0:T(2,128)(2,1)}), bf16[128,2,4096]{2,1,0:T(2,128)(2,1)S(1)}, u32[]{:S(2)}, u32[]{:S(2)}) async-start(bf16[128,2,4096]{2,1,0:T(2,128)(2,1)} %get-tuple-element.7), calls=%async_computation.1 | async-start | bytes 4194304 | tf_op jit(solution)/shard_map/all_to_all | solution.py:10
  184.9 4.1 %reshape.55 = bf16[256,4096]{1,0:T(8,128)(2,1)} reshape(bf16[128,2,4096]{2,1,0:T(2,128)(2,1)} %all_to_all.20) | data formatting | bytes 4194304 | tf_op jit(solution)/shard_map/reshape | solution.py:74
  189.0 5.8 %fusion.8 = f32[256,704]{0,1:T(8,128)} fusion(bf16[256,4096]{1,0:T(8,128)(2,1)} %reshape.55, bf16[1,704,4096]{2,1,0:T(8,128)(2,1)} %param.17), kind=kOutput, calls=%fused_computation.9 | convolution fusion | flops 1476395008 | bytes 8585216 | tf_op jit(solution)/shard_map/dot_general | solution.py:76
  194.9 12.8 %fusion.15 = bf16[256,4096]{1,0:T(8,128)(2,1)} fusion(bf16[1,704,4096]{2,1,0:T(8,128)(2,1)} %param.19, bf16[256,4096]{1,0:T(8,128)(2,1)} %reshape.55, bf16[1,704,4096]{2,1,0:T(8,128)(2,1)} %param.18, f32[256,704]{0,1:T(8,128)} %fusion.8), kind=kOutput, calls=%fused_computation.15 | convolution fusion | flops 2954919936 | bytes 16449536 | tf_op jit(solution)/shard_map/dot_general | solution.py:79
  207.7 4.4 %reshape.56 = bf16[128,2,4096]{2,1,0:T(2,128)(2,1)} reshape(bf16[256,4096]{1,0:T(8,128)(2,1)} %fusion.15) | data formatting | bytes 4194304 | tf_op jit(solution)/shard_map/reshape | solution.py:80
  212.1 10.2 %all-to-all-start.3 = ((bf16[128,2,4096]{2,1,0:T(2,128)(2,1)}), bf16[128,2,4096]{2,1,0:T(2,128)(2,1)}, u32[]{:S(2)}, u32[]{:S(2)}) async-start(bf16[128,2,4096]{2,1,0:T(2,128)(2,1)} %reshape.56), calls=%async_computation.4 | async-start | bytes 4194304 | tf_op jit(solution)/shard_map/all_to_all | solution.py:83
  222.3 2.2 reshape.53
  224.5 6.0 %fusion.10 = f32[256,704]{0,1:T(8,128)} fusion(bf16[256,4096]{1,0:T(8,128)(2,1)} %reshape.53, bf16[1,704,4096]{2,1,0:T(8,128)(2,1)} %param.17), kind=kOutput, calls=%fused_computation.11 | convolution fusion | flops 1476395008 | bytes 8585216 | tf_op jit(solution)/shard_map/dot_general | solution.py:76
  230.5 12.2 %fusion.12 = bf16[256,4096]{1,0:T(8,128)(2,1)} fusion(bf16[1,704,4096]{2,1,0:T(8,128)(2,1)} %param.19, bf16[256,4096]{1,0:T(8,128)(2,1)S(1)} %copy-done.4, bf16[1,704,4096]{2,1,0:T(8,128)(2,1)} %param.18, f32[256,704]{0,1:T(8,128)} %fusion.10), kind=kOutput, calls=%fused_computation.14 | convolution fusion | flops 2954919936 | bytes 16449536 | tf_op jit(solution)/shard_map/dot_general | solution.py:79
  242.7 4.4 %reshape.54 = bf16[128,2,4096]{2,1,0:T(2,128)(2,1)} reshape(bf16[256,4096]{1,0:T(8,128)(2,1)} %fusion.12) | data formatting | bytes 4194304 | tf_op jit(solution)/shard_map/reshape | solution.py:80
  247.1 0.3 all-to-all-done.3
  247.5 10.0 %all-to-all-start.1 = ((bf16[128,2,4096]{2,1,0:T(2,128)(2,1)}), bf16[128,2,4096]{2,1,0:T(2,128)(2,1)}, u32[]{:S(2)}, u32[]{:S(2)}) async-start(bf16[128,2,4096]{2,1,0:T(2,128)(2,1)} %reshape.54), calls=%async_computation.2 | async-start | bytes 4194304 | tf_op jit(solution)/shard_map/all_to_all | solution.py:83
  257.4 0.2 fusion.53
  258.0 24.6 %all-to-all-done.1 = bf16[128,2,4096]{2,1,0:T(2,128)(2,1)} async-done(((bf16[128,2,4096]{2,1,0:T(2,128)(2,1)}), bf16[128,2,4096]{2,1,0:T(2,128)(2,1)}, u32[]{:S(2)}, u32[]{:S(2)}) %all-to-all-start.1) | async-done | bytes 2097184 | tf_op jit(solution)/shard_map/all_to_all | solution.py:83
  282.6 5.7 %pad_maximum_fusion = bf16[128,4,4096]{2,1,0:T(4,128)(2,1)S(1)} fusion(bf16[128,2,4096]{2,1,0:T(2,128)(2,1)} %all-to-all-done.3, bf16[128,2,4096]{2,1,0:T(2,128)(2,1)} %all-to-all-done.1), kind=kLoop, calls=%fused_computation.19 | loop fusion | flops 8388608 | bytes 8388608 | tf_op jit(solution)/shard_map/concatenate | solution.py:20
  288.3 1.3 convert.1
  289.6 3.5 %slice_add_fusion = f32[64,1,4,4096]{3,2,1,0:T(4,128)} fusion(f32[64,2,4,4096]{3,2,1,0:T(4,128)S(1)} %convert.1), kind=kLoop, calls=%fused_computation.18 | loop fusion | flops 1048576 | bytes 12582912 | tf_op jit(solution)/shard_map/add | solution.py:89
  293.1 5.4 %add.43 = f32[256,4096]{1,0:T(8,128)} reshape(f32[64,1,4,4096]{3,2,1,0:T(4,128)} %slice_add_fusion) | data formatting | bytes 8388608 | tf_op jit(solution)/shard_map/add | solution.py:89
  298.5 5.9 %fusion.18 = bf16[128,4096]{1,0:T(8,128)(2,1)} fusion(f32[256,4096]{1,0:T(8,128)} %add.43, bf16[128,4096]{1,0:T(8,128)(2,1)} %reduce-scatter.2.cloned.1.call-done, bf16[128,4096]{1,0:T(8,128)(2,1)S(1)} %copy-done.2, f32[256]{0:T(256)S(1)} %broadcast_in_dim.48, s32[256]{0:T(256)S(1)} %eq.60, pred[256]{0:T(512)(128)(4,1)S(1)} %gt.19), kind=kOutput, calls=%fused_computation.17 | convolution fusion | flops 1613332480 | bytes 7342336 | tf_op jit(solution)/shard_map/dot_general | solution.py:95
  (29 shorter events, 1.0 us)
Async XLA Ops:
  6.5 1.6 copy-start
  6.5 122.7 %reduce-scatter.2.cloned.1.call-start = ((), (), s32[]{:S(2)}) async-start(), calls=%async_computation.5 | async-start | bytes 17825792 | tf_op jit(solution)/shard_map/reduce_scatter | solution.py:32
  17.5 0.7 copy-start.7
  17.5 0.9 copy-start.8
  17.5 111.7 %copy-start.2 = (bf16[128,4096]{1,0:T(8,128)(2,1)S(1)}, bf16[128,4096]{1,0:T(8,128)(2,1)}, u32[]{:S(2)}) copy-start(bf16[128,4096]{1,0:T(8,128)(2,1)} %param.12) | copy-start | bytes 3145732
  17.5 113.4 %copy-start.6 = (f32[4096]{0:T(1024)S(1)}, f32[4096]{0:T(1024)}, u32[]{:S(2)}) copy-start(f32[4096]{0:T(1024)} %param.13) | copy-start | bytes 49156
  129.2 1.8 copy-start.3
  176.0 36.1 %all-to-all-start = ((bf16[128,2,4096]{2,1,0:T(2,128)(2,1)}), bf16[128,2,4096]{2,1,0:T(2,128)(2,1)S(1)}, u32[]{:S(2)}, u32[]{:S(2)}) async-start(bf16[128,2,4096]{2,1,0:T(2,128)(2,1)} %get-tuple-element.7), calls=%async_computation.1 | async-start | bytes 4194304 | tf_op jit(solution)/shard_map/all_to_all | solution.py:10
  212.1 35.4 %all-to-all-start.3 = ((bf16[128,2,4096]{2,1,0:T(2,128)(2,1)}), bf16[128,2,4096]{2,1,0:T(2,128)(2,1)}, u32[]{:S(2)}, u32[]{:S(2)}) async-start(bf16[128,2,4096]{2,1,0:T(2,128)(2,1)} %reshape.56), calls=%async_computation.4 | async-start | bytes 4194304 | tf_op jit(solution)/shard_map/all_to_all | solution.py:83
  224.5 6.0 %copy-start.4 = (bf16[256,4096]{1,0:T(8,128)(2,1)S(1)}, bf16[256,4096]{1,0:T(8,128)(2,1)}, u32[]{:S(2)}) copy-start(bf16[256,4096]{1,0:T(8,128)(2,1)} %reshape.53) | copy-start | bytes 6291460
  247.1 10.3 %copy-start.5 = (f32[64,256]{1,0:T(8,128)S(1)}, f32[64,256]{1,0:T(8,128)}, u32[]{:S(2)}) copy-start(f32[64,256]{1,0:T(8,128)} %param.15) | copy-start | bytes 196612
  247.5 35.1 %all-to-all-start.1 = ((bf16[128,2,4096]{2,1,0:T(2,128)(2,1)}), bf16[128,2,4096]{2,1,0:T(2,128)(2,1)}, u32[]{:S(2)}, u32[]{:S(2)}) async-start(bf16[128,2,4096]{2,1,0:T(2,128)(2,1)} %reshape.54), calls=%async_computation.2 | async-start | bytes 4194304 | tf_op jit(solution)/shard_map/all_to_all | solution.py:83
  293.1 11.4 %copy-start.1 = (bf16[256,4096]{1,0:T(8,128)(2,1)S(1)}, bf16[256,4096]{1,0:T(8,128)(2,1)}, u32[]{:S(2)}) copy-start(bf16[256,4096]{1,0:T(8,128)(2,1)} %param.11) | copy-start | bytes 6291460
Sparse Core Ops, SparseCore 0:
  17.6 111.5 reduce-scatter.1
where the time goes:
time: 317 us; the launch traced here: 311 us
  waiting for transfers between devices  135 us (43%)
  matrix products  54.8 us (17%)
  blocking collectives  34.2 us (11%)
  local copies, waits for them, and re-layouts  32.3 us (10%)
  starting transfers between devices  29.1 us (9%)
  between operations  13.5 us (4%)
  other arithmetic  12.5 us (4%)
    reduce_scatter x1, waiting for transfers between devices, on_device(): lax.psum_scatter(jnp.dot(head_outputs, out_weight, preferred_element_type...  110 us
    all_to_all x1, blocking collectives, moved(): lax.all_to_all(group, axis, split_axis=split_dim, concat_axis=concat_dim,...  34.2 us
    dot_general x2, matrix products, run_expert(): jnp.dot(hidden, w_down[0], preferred_element_type=jnp.float32)  25.1 us
    all_to_all x2, waiting for transfers between devices, serve(): lax.all_to_all(run_expert(received), ('dp', 'tensor'), split_axis=0, conc...  25 us
    all_to_all x2, starting transfers between devices, serve(): lax.all_to_all(run_expert(received), ('dp', 'tensor'), split_axis=0, conc...  20.2 us
    dot_general x2, matrix products, run_expert(): lax.dot_general(flat, w_gate[0], contract, preferred_element_type=jnp.flo...  11.8 us
    dot_general x1, matrix products, on_device(): jnp.dot(head_outputs, out_weight, preferred_element_type=jnp.float32)  9.37 us
    all_to_all x1, starting transfers between devices, moved(): lax.all_to_all(group, axis, split_axis=split_dim, concat_axis=concat_dim,...  8.89 us
  transfers between devices with their start and end apart: 4, of which 3 were waited for; matrix products, arithmetic and copies ran while one was open for 17% of the time, Pallas kernels for 0%

commit v1 on v0

v1 whole, which is shorter than its diff:
```python
import jax
import jax.numpy as jnp
from jax import lax
from jax.sharding import PartitionSpec as P

ROUTE = ("x", "tensor")
BF16 = jnp.bfloat16


def slots_of_block(chosen_pair, gates_pair, first_row, row_count, most):
    local_row = chosen_pair - first_row
    is_mine = (local_row >= 0) & (local_row < row_count)
    capacity_ids = jnp.arange(chosen_pair.shape[1], dtype=jnp.int32)
    earlier = (capacity_ids[:, None] < capacity_ids[None, :]).astype(BF16)
    rank = jnp.dot(is_mine.astype(BF16), earlier, preferred_element_type=jnp.float32)
    matches = is_mine[:, None, :] & (
        rank.astype(jnp.int32)[:, None, :] == jnp.arange(most, dtype=jnp.int32)[None, :, None]
    )
    row = jnp.sum(jnp.where(matches, local_row[:, None, :] + 1, 0), axis=2) - 1
    gate = jnp.sum(jnp.where(matches, gates_pair[:, None, :], 0.0), axis=2)
    return row, gate


def on_device(
    head_outputs, out_weight, residual, norm_gain, chosen, gates, place, w_gate, w_up, w_down
):
    x_count = lax.axis_size("x")
    core_count = lax.axis_size("core")
    tensor_count = lax.axis_size("tensor")
    x_at = lax.axis_index("x")
    core_at = lax.axis_index("core")
    owners = x_count * core_count * tensor_count
    row_count, model_width = residual.shape
    experts = place.shape[0]
    capacity = chosen.shape[1]
    most = 2 * capacity // owners
    swap = [(i, core_count - 1 - i) for i in range(core_count)]

    projected = lax.psum_scatter(
        jnp.dot(head_outputs, out_weight, preferred_element_type=jnp.float32).astype(BF16),
        "tensor",
        scatter_dimension=0,
        tiled=True,
    ).astype(jnp.float32)
    layer_state = residual.astype(jnp.float32) + projected
    scale = lax.rsqrt(jnp.mean(layer_state * layer_state, axis=1, keepdims=True) + 1.0)
    normed = (layer_state * scale * norm_gain[None, :]).astype(BF16)

    by_x = jnp.arange(x_count, dtype=jnp.int32) * core_count + core_at
    pairs = (by_x[:, None] * (tensor_count // 2) + jnp.arange(tensor_count // 2, dtype=jnp.int32)).reshape(-1)
    pair_map = (place[None, :] == pairs[:, None]).astype(jnp.float32)
    chosen_pair = jnp.dot(
        pair_map, chosen.astype(jnp.float32), precision=lax.Precision.HIGHEST
    ).astype(jnp.int32)
    gates_pair = jnp.dot(pair_map, gates, precision=lax.Precision.HIGHEST)
    tensor_at = lax.axis_index("tensor")
    my_first = ((x_at * core_count + core_at) * tensor_count + tensor_at) * row_count
    other_first = ((x_at * core_count + 1 - core_at) * tensor_count + tensor_at) * row_count
    my_row, my_gate = slots_of_block(chosen_pair, gates_pair, my_first, row_count, most)
    other_row, other_gate = slots_of_block(chosen_pair, gates_pair, other_first, row_count, most)
    other_row = jnp.where(other_row >= 0, other_row + row_count, -1)
    units = 2 * most
    slot_row = jnp.concatenate([my_row, other_row], axis=1)
    slot_gate = jnp.concatenate([my_gate, other_gate], axis=1)
    slot_row = jnp.broadcast_to(slot_row[:, None], (experts // 2, 2, units)).reshape(-1)
    slot_gate = jnp.broadcast_to(slot_gate[:, None], (experts // 2, 2, units)).reshape(-1)
    row_ids = jnp.arange(2 * row_count, dtype=jnp.int32)
    selector = (slot_row[:, None] == row_ids[None, :]).astype(BF16)
    combine = jnp.where(slot_row[None, :] == row_ids[:, None], slot_gate[None, :], 0.0)
    combine_high = combine.astype(BF16)
    combine_low = (combine - combine_high.astype(jnp.float32)).astype(BF16)

    both = jnp.concatenate([normed, lax.ppermute(normed, "core", swap)], axis=0)
    outgoing = jnp.dot(selector, both, preferred_element_type=jnp.float32).astype(BF16)
    received = lax.all_to_all(outgoing, ROUTE, split_axis=0, concat_axis=0, tiled=True)

    contract = (((1,), (1,)), ((), ()))
    gate_part = lax.dot_general(received, w_gate[0], contract, preferred_element_type=jnp.float32)
    up_part = lax.dot_general(received, w_up[0], contract, preferred_element_type=jnp.float32)
    hidden = (jax.nn.silu(gate_part) * up_part).astype(BF16)
    result = jnp.dot(hidden, w_down[0], preferred_element_type=jnp.float32).astype(BF16)

    returned = lax.all_to_all(result, ROUTE, split_axis=0, concat_axis=0, tiled=True)
    moe = jnp.dot(combine_high, returned, preferred_element_type=jnp.float32) + jnp.dot(
        combine_low, returned, preferred_element_type=jnp.float32
    )
    from_other = lax.ppermute(moe[row_count:].astype(BF16), "core", swap)
    return (layer_state + (moe[:row_count] + from_other.astype(jnp.float32))).astype(BF16)


def solution(mesh):
    dp, tensor = mesh.devices.shape
    split = jax.sharding.Mesh(mesh.devices.reshape(dp // 2, 2, tensor), ("x", "core", "tensor"))
    rows = P(("x", "core", "tensor"), None)
    weight = P(("x", "core", "tensor"), None, None)
    return jax.shard_map(
        on_device,
        mesh=split,
        in_specs=(
            P(("x", "core"), "tensor"),
            P("tensor", None),
            rows,
            P(),
            P(),
            P(),
            P(),
            weight,
            weight,
            weight,
        ),
        out_specs=rows,
        check_vma=False,
    )
```

time: 317 us -> 305 us (0.962); the launches traced: 311 us -> 305 us
  waiting for transfers between devices: 135 us -> 175 us
  local copies, waits for them, and re-layouts: 32.3 us -> 4.83 us
  blocking collectives: 34.2 us -> 61.3 us
  starting transfers between devices: 29.1 us -> 8.88 us
  matrix products: 54.8 us -> 35.8 us
  other arithmetic: 12.5 us -> 5.32 us
    all_to_all x3 -> x1, waiting for transfers between devices: 25 us -> 60.6 us  [on_device(): lax.all_to_all(result, ROUTE, split_axis=0, concat_axis=0, tiled=True)]
    all_to_all x1, blocking collectives: 34.2 us -> 61.3 us  [on_device(): lax.all_to_all(outgoing, ROUTE, split_axis=0, concat_axis=0, tiled=True)]
    all_to_all x3 -> x1, starting transfers between devices: 29.1 us -> 7.24 us  [on_device(): lax.all_to_all(result, ROUTE, split_axis=0, concat_axis=0, tiled=True)]
    dot_general x7, matrix products: 45.1 us -> 26 us  [the longest x1 14.1 us: on_device(): jnp.dot(hidden, w_down[0], preferred_element_type=jnp.float32).astype(BF16)]
    reshape x4 -> x0, local copies, waits for them, and re-layouts: 15.1 us -> none  [the longest x2 8.78 us: run_expert(): return result.reshape(layout)]
    concatenate x1 -> x2, other arithmetic: 5.71 us -> 0.02 us  [the longest x1 0.01 us: on_device(): slot_row = jnp.concatenate([my_row, other_row], axis=1)]
    add x1, local copies, waits for them, and re-layouts: 5.44 us -> 0.09 us  [on_device(): by_x[:, None] * (tensor_count // 2)]
    broadcast_in_dim x3, local copies, waits for them, and re-layouts: 4.94 us -> 0.13 us  [the longest x1 0.1 us: on_device(): jnp.where(slot_row[None, :] == row_ids[:, None], slot_gate[None, :], 0.0)]
  transfers between devices with their start and end apart: 4 -> 4, of which waited for: 3 -> 4; matrix products, arithmetic and copies ran while one was open for 17% -> 1% of each run, Pallas kernels for 0% -> 0%
where the time goes in v1:
time: 305 us
  waiting for transfers between devices  175 us (57%)
  blocking collectives  61.3 us (20%)
  matrix products  35.8 us (12%)
  between operations  13.6 us (4%)
  starting transfers between devices  8.88 us (3%)
  other arithmetic  5.32 us (2%)
  local copies, waits for them, and re-layouts  4.83 us (2%)
    reduce_scatter x1, waiting for transfers between devices, on_device(): lax.psum_scatter(jnp.dot(head_outputs, out_weight, preferred_element_type...  111 us
    all_to_all x1, blocking collectives, on_device(): lax.all_to_all(outgoing, ROUTE, split_axis=0, concat_axis=0, tiled=True)  61.3 us
    all_to_all x1, waiting for transfers between devices, on_device(): lax.all_to_all(result, ROUTE, split_axis=0, concat_axis=0, tiled=True)  60.6 us
    dot_general x1, matrix products, on_device(): jnp.dot(hidden, w_down[0], preferred_element_type=jnp.float32).astype(BF16)  14.1 us
    dot_general x1, matrix products, on_device(): jnp.dot(head_outputs, out_weight, preferred_element_type=jnp.float32)  9.37 us
    all_to_all x1, starting transfers between devices, on_device(): lax.all_to_all(result, ROUTE, split_axis=0, concat_axis=0, tiled=True)  7.24 us
  transfers between devices with their start and end apart: 4, of which 4 were waited for; matrix products, arithmetic and copies ran while one was open for 1% of the time, Pallas kernels for 0%

profile of v1, /device:TPU:103, one launch (start us, length us, event | category | flops | bytes accessed | tf_op | source)
XLA Modules:
  0.0 304.7 jit_solution(2977485929342620720)
XLA Ops:
  6.5 1.6 copy-done
  8.1 9.4 %convolution_convert_fusion = bf16[2048,4096]{1,0:T(8,128)(2,1)} fusion(bf16[2048,256]{1,0:T(8,128)(2,1)} %param.10, bf16[256,4096]{1,0:T(8,128)(2,1)S(1)} %copy-done), kind=kOutput, calls=%fused_computation | convolution fusion | flops 4303355904 | bytes 19922944 | tf_op jit(solution)/shard_map/dot_general | solution.py:40
  17.6 0.1 add.95
  17.7 0.6 copy-done.6
  18.3 0.2 subtract_add_fusion.1
  18.6 110.6 %reduce-scatter.2.cloned.1.call-done = bf16[128,4096]{1,0:T(8,128)(2,1)} async-done(((bf16[2048,4096]{1,0:T(8,128)(2,1)}), bf16[128,4096]{1,0:T(8,128)(2,1)}) %reduce-scatter.2.cloned.1.call-update) | async-done | bytes 1048592 | tf_op jit(solution)/shard_map/reduce_scatter | solution.py:39
  129.2 1.6 multiply_reduce_fusion
  130.8 1.6 multiply_convert_fusion
  132.5 0.8 collective-permute-start
  133.4 0.2 convolution_convert_fusion.3
  133.5 0.2 convolution_convert_fusion.4
  133.7 0.2 select_reduce_fusion.2
  133.9 0.1 copy.13
  134.0 0.1 eq.76
  134.1 1.5 collective-permute-done
  135.6 1.3 fusion.8
  136.9 61.3 %all_to_all.24 = bf16[64,8,4096]{2,1,0:T(8,128)(2,1)S(1)} all-to-all(bf16[64,8,4096]{2,1,0:T(8,128)(2,1)S(1)} %fusion.8), channel_id=1, replica_groups=mesh['x'=4,'core'=2,'tensor'=16] {'x','tensor'}, dimensions={0} | all-to-all | bytes 8388608 | tf_op jit(solution)/shard_map/all_to_all | solution.py:75
  198.2 2.0 copy-done.4
  200.2 3.2 %fusion.3 = f32[512,704]{0,1:T(8,128)S(1)} fusion(bf16[1,704,4096]{2,1,0:T(8,128)(2,1)S(1)} %bitcast.43, bf16[64,8,4096]{2,1,0:T(8,128)(2,1)S(1)} %all_to_all.24), kind=kOutput, calls=%fused_computation.6 | convolution fusion | flops 2952790016 | bytes 11403264 | tf_op jit(solution)/shard_map/dot_general | solution.py:78
  203.4 14.1 %fusion.5 = bf16[64,8,4096]{2,1,0:T(8,128)(2,1)} fusion(bf16[1,704,4096]{2,1,0:T(8,128)(2,1)} %param.19, bf16[1,704,4096]{2,1,0:T(8,128)(2,1)} %param.18, bf16[64,8,4096]{2,1,0:T(8,128)(2,1)} %copy-done.4, f32[512,704]{0,1:T(8,128)S(1)} %fusion.3), kind=kOutput, calls=%fused_computation.8 | convolution fusion | flops 5909839872 | bytes 21364736 | tf_op jit(solution)/shard_map/dot_general | solution.py:81
  217.4 7.2 %all-to-all-start.1 = ((bf16[64,8,4096]{2,1,0:T(8,128)(2,1)}), bf16[64,8,4096]{2,1,0:T(8,128)(2,1)}, u32[]{:S(2)}, u32[]{:S(2)}) async-start(bf16[64,8,4096]{2,1,0:T(8,128)(2,1)} %fusion.5), calls=%async_computation.2 | async-start | bytes 8388608 | tf_op jit(solution)/shard_map/all_to_all | solution.py:83
  224.7 0.2 fusion.45
  224.9 0.1 select_reduce_fusion.1
  225.1 0.1 copy.14
  225.1 0.1 broadcast_in_dim.90
  225.3 60.6 %all-to-all-done.1 = bf16[64,8,4096]{2,1,0:T(8,128)(2,1)} async-done(((bf16[64,8,4096]{2,1,0:T(8,128)(2,1)}), bf16[64,8,4096]{2,1,0:T(8,128)(2,1)}, u32[]{:S(2)}, u32[]{:S(2)}) %all-to-all-start.1) | async-done | bytes 4194336 | tf_op jit(solution)/shard_map/all_to_all | solution.py:83
  285.9 3.4 %fusion.10 = f32[256,4096]{1,0:T(8,128)S(1)} fusion(bf16[64,8,4096]{2,1,0:T(8,128)(2,1)} %all-to-all-done.1, f32[512]{0:T(512)S(1)} %broadcast_in_dim.90, s32[512]{0:T(512)S(1)} %eq.76), kind=kOutput, calls=%fused_computation.12 | convolution fusion | flops 1074003968 | bytes 8392704 | tf_op jit(solution)/shard_map/dot_general | solution.py:84
  289.3 3.7 %convolution_add_fusion = f32[256,4096]{1,0:T(8,128)S(1)} fusion(f32[256,4096]{1,0:T(8,128)S(1)} %fusion.10, bf16[64,8,4096]{2,1,0:T(8,128)(2,1)} %all-to-all-done.1, f32[512]{0:T(512)S(1)} %broadcast_in_dim.90, s32[512]{0:T(512)S(1)} %eq.76), kind=kOutput, calls=%fused_computation.10 | convolution fusion | flops 1075576832 | bytes 12587008 | tf_op jit(solution)/shard_map/dot_general | solution.py:84
  293.1 0.1 slice.17
  293.2 0.8 collective-permute-start.1
  294.0 2.3 collective-permute-done.1
  296.3 1.5 fusion.15
  (34 shorter events, 0.2 us)
Async XLA Ops:
  6.5 1.6 copy-start
  6.5 122.6 %reduce-scatter.2.cloned.1.call-start = ((), (), s32[]{:S(2)}) async-start(), calls=%async_computation.3 | async-start | bytes 17825792 | tf_op jit(solution)/shard_map/reduce_scatter | solution.py:39
  17.5 0.8 copy-start.6
  17.5 0.8 copy-start.8
  17.5 111.7 %copy-start.2 = (bf16[128,4096]{1,0:T(8,128)(2,1)S(1)}, bf16[128,4096]{1,0:T(8,128)(2,1)}, u32[]{:S(2)}) copy-start(bf16[128,4096]{1,0:T(8,128)(2,1)} %param.12) | copy-start | bytes 3145732
  17.5 113.3 %copy-start.7 = (f32[4096]{0:T(1024)S(1)}, f32[4096]{0:T(1024)}, u32[]{:S(2)}) copy-start(f32[4096]{0:T(1024)} %param.13) | copy-start | bytes 49156
  132.5 3.1 %collective-permute-start = (bf16[128,4096]{1,0:T(8,128)(2,1)S(1)}, bf16[128,4096]{1,0:T(8,128)(2,1)S(1)}, u32[]{:S(2)}, u32[]{:S(2)}) collective-permute-start(bf16[128,4096]{1,0:T(8,128)(2,1)S(1)} %multiply_convert_fusion), channel_id=1, source_target_pairs={{0,16},{16,0},{1,17},{17,1},{2,18},{18,2},{3,19},{19,3},{4,20},{20... | collective-permute-start | bytes 3145736 | tf_op jit(solution)/shard_map/ppermute | solution.py:73
  135.6 64.6 %slice-start = ((s8[5767168]{0:T(1024)(128)(4,1)}), s8[4194304]{0:T(1024)(128)(4,1)S(1)}, s32[]{:S(2)}) async-start(s8[5767168]{0:T(1024)(128)(4,1)} %bitcast.42), calls=%async_computation.4 | async-start | bytes 8388608
  136.9 63.3 %slice-start.1 = ((s8[5767168]{0:T(1024)(128)(4,1)}), s8[1572864]{0:T(1024)(128)(4,1)S(1)}, s32[]{:S(2)}) async-start(s8[5767168]{0:T(1024)(128)(4,1)} %bitcast.42), calls=%async_computation.5 | async-start | bytes 3145728
  198.2 2.0 copy-start.4
  217.4 7.3 %copy-start.5 = (f32[64,256]{1,0:T(8,128)S(1)}, f32[64,256]{1,0:T(8,128)}, u32[]{:S(2)}) copy-start(f32[64,256]{1,0:T(8,128)} %param.15) | copy-start | bytes 196612
  217.4 68.4 %all-to-all-start.1 = ((bf16[64,8,4096]{2,1,0:T(8,128)(2,1)}), bf16[64,8,4096]{2,1,0:T(8,128)(2,1)}, u32[]{:S(2)}, u32[]{:S(2)}) async-start(bf16[64,8,4096]{2,1,0:T(8,128)(2,1)} %fusion.5), calls=%async_computation.2 | async-start | bytes 8388608 | tf_op jit(solution)/shard_map/all_to_all | solution.py:83
  289.3 7.0 %copy-start.3 = (bf16[128,4096]{1,0:T(8,128)(2,1)S(1)}, bf16[128,4096]{1,0:T(8,128)(2,1)}, u32[]{:S(2)}) copy-start(bf16[128,4096]{1,0:T(8,128)(2,1)} %reduce-scatter.2.cloned.1.call-done) | copy-start | bytes 3145732
  289.3 8.5 %copy-start.1 = (bf16[256,4096]{1,0:T(8,128)(2,1)S(1)}, bf16[256,4096]{1,0:T(8,128)(2,1)}, u32[]{:S(2)}) copy-start(bf16[256,4096]{1,0:T(8,128)(2,1)} %param.11) | copy-start | bytes 6291460
  293.2 3.1 %collective-permute-start.1 = (bf16[128,4096]{1,0:T(8,128)(2,1)S(1)}, bf16[128,4096]{1,0:T(8,128)(2,1)S(1)}, u32[]{:S(2)}, u32[]{:S(2)}) collective-permute-start(bf16[128,4096]{1,0:T(8,128)(2,1)S(1)} %slice.17), channel_id=1, source_target_pairs={{0,16},{16,0},{1,17},{17,1},{2,18},{18,2},{3,19},{19,3},{4,20},{20... | collective-permute-start | bytes 3145736 | tf_op jit(solution)/shard_map/ppermute | solution.py:87
Sparse Core Ops, SparseCore 0:
  17.7 111.4 reduce-scatter.1
